TPU v7x, 32 devices: a whole 2x2x4 slice. The times are simulated.
32 devices in a mesh: bank: 8 (over z, core), zero: 4 (over y, x).
Axes of the slice: x: 2, y: 2, z: 4, core: 2. Of those that a mesh axis runs over, the one named last changes fastest.
Arguments:
- master_gate: float32 [64, 2048, 1408], P('bank', 'zero'), may hold values from -0.1875 to 0.1875
- master_up: float32 [64, 2048, 1408], P('bank', 'zero'), may hold values from -0.1875 to 0.1875
- master_down: float32 [64, 1408, 2048], P('bank', None, 'zero'), may hold values from -0.21875 to 0.21875
- router_weight: float32 [2048, 64], P('zero', 'bank'), may hold values from -0.125 to 0.125
- router_gain: float32 [2048], P('zero'), may hold values from 0.25 to 1.75
Outputs:
- final_gate: bfloat16 [64, 2048, 1408], P('bank', None, 'zero')
- final_up: bfloat16 [64, 2048, 1408], P('bank', None, 'zero')
- final_down: bfloat16 [64, 1408, 2048], P('bank', 'zero')
- scale_gate: float32 [64, 1408], P('bank', 'zero')
- scale_up: float32 [64, 1408], P('bank', 'zero')
- scale_down: float32 [64, 1408], P('bank', 'zero')
- serve_router: bfloat16 [2048, 64], replicated
All inputs are finite; a program needn't handle non-finite values. Where the computation divides by a largest or mean magnitude, that divisor is 1e-20 or more.
Results may differ from a plain program's by a relative error of at most 0.0013.
Values may be sent and summed in bfloat16 or wider, within the bound.
A program may use at most 192 MiB of HBM per device.

v0:
```python
import jax
import jax.numpy as jnp
from jax import lax
from jax.sharding import PartitionSpec as P


def exchange(wide, scale, parts):
    experts, rows, width = wide.shape
    narrow = (wide / scale[:, :, None]).astype(jnp.bfloat16)
    cut = narrow.reshape(experts, parts, rows // parts, width).transpose(1, 0, 2, 3)
    return lax.all_to_all(cut, "zero", split_axis=0, concat_axis=0, tiled=True), cut


def merged(blocks):
    return jnp.concatenate([blocks[p] for p in range(blocks.shape[0])], axis=2)


def local(parts, master_gate, master_up, master_down, router_weight, router_gain):
    experts, rows, inner = master_gate.shape
    d_model = rows * parts
    sums = jnp.stack(
        [
            jnp.sum(jnp.abs(master_gate), axis=1),
            jnp.sum(jnp.abs(master_up), axis=1),
            jnp.sum(jnp.abs(master_down), axis=2),
        ]
    )
    part_router = (router_weight * router_gain[:, None]).astype(jnp.bfloat16).T
    router = lax.all_gather(part_router, ("bank", "zero"), axis=0, tiled=False)
    sums, router = lax.optimization_barrier((sums, router))
    every = lax.all_gather(sums, "zero", axis=0, tiled=False)
    scales = jnp.sum(every, axis=0) / d_model
    router = router.reshape(-1, parts, experts, rows).transpose(0, 2, 1, 3)
    serve_router = router.reshape(-1, d_model).T

    got_down, cut = exchange(master_down, scales[2], parts)
    master_gate, cut = lax.optimization_barrier((master_gate, cut))
    got_gate, cut = exchange(master_gate.transpose(0, 2, 1), scales[0], parts)
    master_up, cut = lax.optimization_barrier((master_up, cut))
    got_up, cut = exchange(master_up.transpose(0, 2, 1), scales[1], parts)

    final_down = merged(got_down)
    final_gate = merged(got_gate).transpose(0, 2, 1)
    final_up = merged(got_up).transpose(0, 2, 1)
    own = lax.dynamic_slice_in_dim(
        scales, lax.axis_index("zero") * (inner // parts), inner // parts, axis=2
    )
    return (final_gate, final_up, final_down, own[0], own[1], own[2], serve_router)


def solution(mesh):
    placed = (
        P("bank", "zero", None),
        P("bank", "zero", None),
        P("bank", None, "zero"),
        P("zero", "bank"),
        P("zero"),
    )
    parts = mesh.shape["zero"]
    return jax.shard_map(
        lambda *arrays: local(parts, *arrays),
        mesh=mesh,
        in_specs=placed,
        out_specs=(
            P("bank", None, "zero"),
            P("bank", None, "zero"),
            P("bank", "zero", None),
            P("bank", "zero"),
            P("bank", "zero"),
            P("bank", "zero"),
            P(),
        ),
        check_vma=False,
    )
```

profile of v0, /device:TPU:0, one launch (start us, length us, event | category | flops | bytes accessed | tf_op | source)
XLA Modules:
  0.0 522.6 jit_solution(1423111512351173173)
XLA Ops:
  0.7 10.4 %abs_reduce_fusion.2 = f32[8,1408]{1,0:T(8,128)S(1)} fusion(f32[8,512,1408]{2,1,0:T(8,128)} %param.5), kind=kLoop, calls=%fused_computation.5 | loop fusion | flops 11523072 | bytes 23113728 | tf_op jit(solution)/shard_map/reduce_sum | solution.py:23
  11.1 11.0 %abs_reduce_fusion.1 = f32[8,1408]{1,0:T(8,128)S(1)} fusion(f32[8,512,1408]{2,1,0:T(8,128)} %param.6), kind=kLoop, calls=%fused_computation.4 | loop fusion | flops 11523072 | bytes 23113728 | tf_op jit(solution)/shard_map/reduce_sum | solution.py:24
  26.1 71.1 %all-gather = bf16[256,512]{1,0:T(8,128)(2,1)S(1)} all-gather(bf16[8,512]{1,0:T(8,128)(2,1)S(1)} %fusion), channel_id=2, replica_groups=mesh['bank'=8,'zero'=4] {'bank','zero'}, dimensions={0}, use_global_device_ids=true | all-gather | bytes 270336 | tf_op jit(solution)/shard_map/all_gather | solution.py:29
  97.2 8.6 %all-gather.1 = f32[12,8,1408]{2,1,0:T(8,128)S(1)} all-gather(f32[3,8,1408]{2,1,0:T(8,128)S(1)} %pad_maximum_fusion.1), channel_id=3, replica_groups=mesh['bank'=8,'zero'=4] {'zero'}, dimensions={0}, use_global_device_ids=true | all-gather | bytes 675840 | tf_op jit(solution)/shard_map/all_gather | solution.py:31
  105.9 9.4 %divide_convert_fusion.2 = bf16[8,1408,512]{2,1,0:T(8,128)(2,1)S(1)} fusion(f32[8,1408,512]{2,1,0:T(8,128)} %param.7, f32[8,1408]{1,0:T(8,128)S(1)} %get-tuple-element.32), kind=kLoop, calls=%fused_computation.2 | loop fusion | flops 11534336 | bytes 34648064 | tf_op jit(solution)/shard_map/convert_element_type | solution.py:9
  115.4 5.0 copy.27
  120.4 6.2 %all-to-all-start.2 = ((bf16[4,8,352,512]{3,2,1,0:T(8,128)(2,1)}), bf16[4,8,352,512]{3,2,1,0:T(8,128)(2,1)}, u32[]{:S(2)}, u32[]{:S(2)}) async-start(bf16[4,8,352,512]{3,2,1,0:T(8,128)(2,1)} %copy.27), calls=%async_computation.2 | async-start | bytes 23068672 | tf_op jit(solution)/shard_map/all_to_all | solution.py:11
  126.6 23.4 %copy.23 = f32[8,512,1408]{1,2,0:T(8,128)} copy(f32[8,512,1408]{2,1,0:T(8,128)} %param.5) | data formatting | bytes 46137344 | tf_op jit(solution)/shard_map/optimization_barrier | solution.py:37
  150.0 9.4 %divide_convert_fusion.1 = bf16[8,512,1408]{1,2,0:T(8,128)(2,1)S(1)} fusion(f32[8,512,1408]{1,2,0:T(8,128)} %copy.23, f32[8,1408]{1,0:T(8,128)S(1)} %get-tuple-element.31), kind=kLoop, calls=%fused_computation.1 | loop fusion | flops 11534336 | bytes 34648064 | tf_op jit(solution)/shard_map/convert_element_type | solution.py:9
  159.4 5.0 copy.24
  164.4 82.9 %all-to-all-done.2 = bf16[4,8,352,512]{3,2,1,0:T(8,128)(2,1)} async-done(((bf16[4,8,352,512]{3,2,1,0:T(8,128)(2,1)}), bf16[4,8,352,512]{3,2,1,0:T(8,128)(2,1)}, u32[]{:S(2)}, u32[]{:S(2)}) %all-to-all-start.2) | async-done | bytes 11534368 | tf_op jit(solution)/shard_map/all_to_all | solution.py:11
  247.4 6.2 %all-to-all-start = ((bf16[4,8,352,512]{3,2,1,0:T(8,128)(2,1)}), bf16[4,8,352,512]{3,2,1,0:T(8,128)(2,1)}, u32[]{:S(2)}, u32[]{:S(2)}) async-start(bf16[4,8,352,512]{3,2,1,0:T(8,128)(2,1)} %copy.24), calls=%async_computation | async-start | bytes 23068672 | tf_op jit(solution)/shard_map/all_to_all | solution.py:11
  253.6 23.4 %copy.25 = f32[8,512,1408]{1,2,0:T(8,128)} copy(f32[8,512,1408]{2,1,0:T(8,128)} %param.6) | data formatting | bytes 46137344 | tf_op jit(solution)/shard_map/optimization_barrier | solution.py:39
  277.0 9.4 %divide_convert_fusion = bf16[8,512,1408]{1,2,0:T(8,128)(2,1)S(1)} fusion(f32[8,512,1408]{1,2,0:T(8,128)} %copy.25, f32[8,1408]{1,0:T(8,128)S(1)} %get-tuple-element.30), kind=kLoop, calls=%fused_computation | loop fusion | flops 11534336 | bytes 34648064 | tf_op jit(solution)/shard_map/convert_element_type | solution.py:9
  286.4 5.0 copy.26
  291.5 88.6 %all-to-all-done = bf16[4,8,352,512]{3,2,1,0:T(8,128)(2,1)} async-done(((bf16[4,8,352,512]{3,2,1,0:T(8,128)(2,1)}), bf16[4,8,352,512]{3,2,1,0:T(8,128)(2,1)}, u32[]{:S(2)}, u32[]{:S(2)}) %all-to-all-start) | async-done | bytes 11534368 | tf_op jit(solution)/shard_map/all_to_all | solution.py:11
  380.0 6.2 %all-to-all-start.1 = ((bf16[4,8,352,512]{3,2,1,0:T(8,128)(2,1)}), bf16[4,8,352,512]{3,2,1,0:T(8,128)(2,1)}, u32[]{:S(2)}, u32[]{:S(2)}) async-start(bf16[4,8,352,512]{3,2,1,0:T(8,128)(2,1)} %copy.26), calls=%async_computation.1 | async-start | bytes 23068672 | tf_op jit(solution)/shard_map/all_to_all | solution.py:11
  386.9 4.9 slice_bitcast_fusion.3
  391.8 4.9 slice_bitcast_fusion.11
  396.7 5.2 pad_maximum_fusion
  401.9 5.2 maximum_bitcast_fusion
  407.1 104.8 %all-to-all-done.1 = bf16[4,8,352,512]{3,2,1,0:T(8,128)(2,1)} async-done(((bf16[4,8,352,512]{3,2,1,0:T(8,128)(2,1)}), bf16[4,8,352,512]{3,2,1,0:T(8,128)(2,1)}, u32[]{:S(2)}, u32[]{:S(2)}) %all-to-all-start.1) | async-done | bytes 11534368 | tf_op jit(solution)/shard_map/all_to_all | solution.py:11
  511.9 4.9 slice_bitcast_fusion.7
  516.7 5.2 maximum_bitcast_fusion.1
  (25 shorter events, 5.4 us)
Async XLA Ops:
  0.6 21.4 %slice-start = ((s8[23068672]{0:T(1024)(128)(4,1)}), s8[4194304]{0:T(1024)(128)(4,1)S(1)}, s32[]{:S(2)}) async-start(s8[23068672]{0:T(1024)(128)(4,1)} %bitcast.67), calls=%async_computation.3 | async-start | bytes 8388608
  0.6 21.4 %slice-start.1 = ((s8[23068672]{0:T(1024)(128)(4,1)}), s8[4194304]{0:T(1024)(128)(4,1)S(1)}, s32[]{:S(2)}) async-start(s8[23068672]{0:T(1024)(128)(4,1)} %bitcast.67), calls=%async_computation.4 | async-start | bytes 8388608
  0.7 21.4 %slice-start.2 = ((s8[23068672]{0:T(1024)(128)(4,1)}), s8[4194304]{0:T(1024)(128)(4,1)S(1)}, s32[]{:S(2)}) async-start(s8[23068672]{0:T(1024)(128)(4,1)} %bitcast.67), calls=%async_computation.5 | async-start | bytes 8388608
  11.1 11.0 %slice-start.3 = ((s8[23068672]{0:T(1024)(128)(4,1)}), s8[4194304]{0:T(1024)(128)(4,1)S(1)}, s32[]{:S(2)}) async-start(s8[23068672]{0:T(1024)(128)(4,1)} %bitcast.67), calls=%async_computation.6 | async-start | bytes 8388608
  11.1 11.0 %slice-start.4 = ((s8[23068672]{0:T(1024)(128)(4,1)}), s8[4194304]{0:T(1024)(128)(4,1)S(1)}, s32[]{:S(2)}) async-start(s8[23068672]{0:T(1024)(128)(4,1)} %bitcast.67), calls=%async_computation.7 | async-start | bytes 8388608
  11.1 11.0 %slice-start.5 = ((s8[23068672]{0:T(1024)(128)(4,1)}), s8[2097152]{0:T(1024)(128)(4,1)S(1)}, s32[]{:S(2)}) async-start(s8[23068672]{0:T(1024)(128)(4,1)} %bitcast.67), calls=%async_computation.8 | async-start | bytes 4194304
  22.1 4.0 copy-start
  22.1 4.0 copy-start.1
  120.4 127.0 %all-to-all-start.2 = ((bf16[4,8,352,512]{3,2,1,0:T(8,128)(2,1)}), bf16[4,8,352,512]{3,2,1,0:T(8,128)(2,1)}, u32[]{:S(2)}, u32[]{:S(2)}) async-start(bf16[4,8,352,512]{3,2,1,0:T(8,128)(2,1)} %copy.27), calls=%async_computation.2 | async-start | bytes 23068672 | tf_op jit(solution)/shard_map/all_to_all | solution.py:11
  247.4 132.7 %all-to-all-start = ((bf16[4,8,352,512]{3,2,1,0:T(8,128)(2,1)}), bf16[4,8,352,512]{3,2,1,0:T(8,128)(2,1)}, u32[]{:S(2)}, u32[]{:S(2)}) async-start(bf16[4,8,352,512]{3,2,1,0:T(8,128)(2,1)} %copy.24), calls=%async_computation | async-start | bytes 23068672 | tf_op jit(solution)/shard_map/all_to_all | solution.py:11
  380.0 131.8 %all-to-all-start.1 = ((bf16[4,8,352,512]{3,2,1,0:T(8,128)(2,1)}), bf16[4,8,352,512]{3,2,1,0:T(8,128)(2,1)}, u32[]{:S(2)}, u32[]{:S(2)}) async-start(bf16[4,8,352,512]{3,2,1,0:T(8,128)(2,1)} %copy.26), calls=%async_computation.1 | async-start | bytes 23068672 | tf_op jit(solution)/shard_map/all_to_all | solution.py:11
where the time goes:
time: 524 us; the launch traced here: 523 us
  waiting for transfers between devices  276 us (53%)
  blocking collectives  79.7 us (15%)
  local copies, waits for them, and re-layouts  77.9 us (15%)
  other arithmetic  69.2 us (13%)
  starting transfers between devices  18.6 us (4%)
    all_to_all x3, waiting for transfers between devices, exchange(): lax.all_to_all(cut, 'zero', split_axis=0, concat_axis=0, tiled=True)  276 us
    all_gather x1, blocking collectives, local(): router = lax.all_gather(part_router, ('bank', 'zero'), axis=0, tiled=False)  71.1 us
    convert_element_type x3, other arithmetic, exchange(): narrow = (wide / scale[:, :, None]).astype(jnp.bfloat16)  28.3 us
    optimization_barrier x1, local copies, waits for them, and re-layouts, local(): master_gate, cut = lax.optimization_barrier((master_gate, cut))  23.4 us
    optimization_barrier x1, local copies, waits for them, and re-layouts, local(): master_up, cut = lax.optimization_barrier((master_up, cut))  23.4 us
    all_to_all x3, starting transfers between devices, exchange(): lax.all_to_all(cut, 'zero', split_axis=0, concat_axis=0, tiled=True)  18.6 us
    transpose x3, local copies, waits for them, and re-layouts, exchange(): narrow.reshape(experts, parts, rows // parts, width).transpose(1, 0, 2, 3)  15.1 us
    squeeze x3, local copies, waits for them, and re-layouts, merged(): return jnp.concatenate([blocks[p] for p in range(blocks.shape[0])], axis=2)  14.6 us
  transfers between devices with their start and end apart: 3, of which 3 were waited for; matrix products, arithmetic and copies ran while one was open for 18% of the time, Pallas kernels for 0%

commit v1 on v0

v1 whole, which is shorter than its diff:
```python
import functools
import math

import jax
import jax.numpy as jnp
from jax import lax
from jax.experimental import pallas as pl
from jax.experimental.pallas import tpu as pltpu
from jax.sharding import PartitionSpec as P

LANES = 128
DOWN, GATE, UP = range(3)
MESH = pl.DeviceIdType.MESH


def span(index, size):
    return pl.ds(pl.multiple_of(index * size, size), size)


def row_sums_across(wide, put):
    def one(j, _):
        put(j, jnp.sum(jnp.abs(wide[:, span(j, LANES)]), axis=0, keepdims=True))
        return 0

    lax.fori_loop(0, wide.shape[1] // LANES, one, 0)


def row_sums_along(wide, put):
    def one(j, _):
        block = jnp.abs(wide[span(j, LANES), :])
        total = block[:, :LANES]
        for k in range(1, block.shape[1] // LANES):
            total = total + block[:, k * LANES : (k + 1) * LANES]
        put(j, jnp.sum(total.T, axis=0, keepdims=True))
        return 0

    lax.fori_loop(0, wide.shape[0] // LANES, one, 0)


def exchange_kernel(
    parts,
    kept,
    gate,
    up,
    down,
    weight,
    gain,
    out_gate,
    out_up,
    out_down,
    cut,
    out_strip,
    scales,
    wide_gate,
    wide_up,
    wide_down,
    narrow,
    columns_of,
    sums,
    weight_now,
    gain_now,
    strip,
    load_sem,
    sum_send,
    sum_recv,
    data_send,
    data_recv,
    own_sem,
    cut_sem,
    router_load,
    part_send,
    part_recv,
    strip_sem,
):
    me = lax.axis_index("zero")
    experts, rows, inner = gate.shape
    width = inner // parts
    chunk = math.gcd(width, 32)
    d_model = rows * parts
    source = {DOWN: down, GATE: gate, UP: up}
    wide = {DOWN: wide_down, GATE: wide_gate, UP: wide_up}
    result = {DOWN: out_down, GATE: out_gate, UP: out_up}
    peers = [lax.rem(me + k, parts) for k in range(1, parts)]

    def load(m, e):
        slot = lax.rem(e, 2)
        return pltpu.make_async_copy(source[m].at[e], wide[m].at[slot], load_sem.at[m, slot])

    def sum_copy(m, e, k, sender):
        return pltpu.make_async_remote_copy(
            src_ref=sums.at[m, e, sender],
            dst_ref=sums.at[m, e, sender],
            send_sem=sum_send.at[m, k],
            recv_sem=sum_recv.at[m, e, sender],
            device_id={"zero": peers[k]},
            device_id_type=MESH,
        )

    def block_copy(m, e, k, sender):
        slot = lax.rem(e, 2)
        return pltpu.make_async_remote_copy(
            src_ref=narrow.at[m, slot, span(peers[k], width), :],
            dst_ref=result[m].at[e, :, span(sender, rows)],
            send_sem=data_send.at[m, slot, k],
            recv_sem=data_recv.at[m, e, sender],
            device_id={"zero": peers[k]},
            device_id_type=MESH,
        )

    def own_copy(m, e):
        slot = lax.rem(e, 2)
        return pltpu.make_async_copy(
            narrow.at[m, slot, span(me, width), :],
            result[m].at[e, :, span(me, rows)],
            own_sem.at[m, slot],
        )

    def cut_copy(e, p):
        slot = lax.rem(e, 2)
        return pltpu.make_async_copy(
            narrow.at[DOWN, slot, pl.ds(p * width, width), :],
            cut.at[p, e - kept],
            cut_sem.at[slot, p],
        )

    def begin(m, e, ready=lambda: None):
        load(m, e).wait()
        slot = lax.rem(e, 2)
        if m != UP:
            pl.when(e < 2)(lambda: load(m + 1, e).start())
        elif experts > 1:
            pl.when(e < 1)(lambda: load(DOWN, e + 1).start())

        def put(j, value):
            sums[m, e, me, :, span(j, LANES)] = value

        (row_sums_along if m == DOWN else row_sums_across)(wide[m].at[slot], put)
        ready()
        for k in range(parts - 1):
            sum_copy(m, e, k, me).start()

    def sent(m, e):
        def remote():
            for k in range(parts - 1):
                block_copy(m, e, k, me).wait_send()
            own_copy(m, e).wait()

        if m != DOWN:
            remote()
            return
        pl.when(e < kept)(remote)

        @pl.when(e >= kept)
        def _():
            for p in range(parts):
                cut_copy(e, p).wait()

    def finish(m, e):
        slot = lax.rem(e, 2)
        for k in range(parts - 1):
            sum_copy(m, e, k, me).wait_send()
            sum_copy(m, e, k, peers[k]).wait_recv()
        pl.when(e >= 2)(lambda: sent(m, e - 2))
        wide_now, narrow_now = wide[m].at[slot], narrow.at[m, slot]

        def inverse_of(columns):
            total = sums[m, e, 0, :, columns]
            for p in range(1, parts):
                total = total + sums[m, e, p, :, columns]
            scale = total / d_model
            scales[m, e, :, columns] = scale
            return 1.0 / scale

        if m == DOWN:

            def by_row(j, _):
                columns = span(j, LANES)
                inverse = jnp.broadcast_to(inverse_of(columns), (LANES, LANES))
                columns_of[columns, :] = inverse.T
                return 0

            lax.fori_loop(0, inner // LANES, by_row, 0, unroll=True)

            def scaled(p):
                def one(c, _):
                    at = pl.ds(pl.multiple_of(p * width + c * chunk, chunk), chunk)
                    inverse = columns_of[at, :]
                    for i in range(rows // LANES):
                        lanes = pl.ds(i * LANES, LANES)
                        narrow_now[at, lanes] = (wide_now[at, lanes] * inverse).astype(jnp.bfloat16)
                    return 0

                lax.fori_loop(0, width // chunk, one, 0)

            for k in range(parts - 1):
                scaled(peers[k])
                pl.when(e < kept)(lambda: block_copy(DOWN, e, k, me).start())
            scaled(me)
            pl.when(e < kept)(lambda: own_copy(DOWN, e).start())

            @pl.when(e >= kept)
            def _():
                for p in range(parts):
                    cut_copy(e, p).start()

        else:

            def one(j, _):
                columns = span(j, LANES)
                inverse = inverse_of(columns)
                for i in range(rows // LANES):
                    at = pl.ds(i * LANES, LANES)
                    block = wide_now[at, columns] * inverse
                    narrow_now[columns, at] = block.T.astype(jnp.bfloat16)
                return 0

            lax.fori_loop(0, inner // LANES, one, 0)
            for k in range(parts - 1):
                block_copy(m, e, k, me).start()
            own_copy(m, e).start()
        pl.when(e + 2 < experts)(lambda: load(m, e + 2).start())

    def part_copy(k, sender):
        return pltpu.make_async_remote_copy(
            src_ref=strip.at[:, span(sender, rows)],
            dst_ref=strip.at[:, span(sender, rows)],
            send_sem=part_send.at[k],
            recv_sem=part_recv.at[sender],
            device_id={"zero": peers[k]},
            device_id_type=MESH,
        )

    router_loads = [
        pltpu.make_async_copy(weight, weight_now, router_load.at[0]),
        pltpu.make_async_copy(gain, gain_now, router_load.at[1]),
    ]

    load(DOWN, 0).start()
    for copy in router_loads:
        copy.start()
    barrier = pltpu.get_barrier_semaphore()
    for peer in peers:
        pl.semaphore_signal(barrier, inc=1, device_id={"zero": peer}, device_id_type=MESH)
    begin(DOWN, 0, lambda: pl.semaphore_wait(barrier, parts - 1))
    begin(GATE, 0)
    for copy in router_loads:
        copy.wait()
    strip[:, span(me, rows)] = (weight_now[...] * gain_now[...]).astype(jnp.bfloat16)
    for k in range(parts - 1):
        part_copy(k, me).start()

    def step(e, _):
        more = e + 1 < experts
        finish(DOWN, e)
        begin(UP, e)
        pl.when(more)(lambda: begin(DOWN, e + 1))
        finish(GATE, e)
        pl.when(more)(lambda: begin(GATE, e + 1))
        finish(UP, e)
        return 0

    lax.fori_loop(0, experts, step, 0)

    for m in (DOWN, GATE, UP):
        for e in range(max(experts - 2, 0), experts):
            sent(m, jnp.int32(e))

    def arrived(e, _):
        for k in range(parts - 1):
            for m in (GATE, UP):
                block_copy(m, e, k, peers[k]).wait_recv()

            @pl.when(e < kept)
            def _():
                block_copy(DOWN, e, k, peers[k]).wait_recv()

        return 0

    lax.fori_loop(0, experts, arrived, 0)
    for k in range(parts - 1):
        part_copy(k, me).wait_send()
        part_copy(k, peers[k]).wait_recv()
    strip_copy = pltpu.make_async_copy(strip, out_strip, strip_sem)
    strip_copy.start()
    strip_copy.wait()


def exchange(parts, kept, gate, up, down, weight, gain):
    experts, rows, inner = gate.shape
    width, d_model = inner // parts, rows * parts
    left = experts - kept
    any_space = pl.BlockSpec(memory_space=pl.ANY)
    narrow = jnp.bfloat16
    dma = pltpu.SemaphoreType.DMA
    return pl.pallas_call(
        functools.partial(exchange_kernel, parts, kept),
        out_shape=(
            jax.ShapeDtypeStruct((experts, width, d_model), narrow),
            jax.ShapeDtypeStruct((experts, width, d_model), narrow),
            jax.ShapeDtypeStruct((kept, width, d_model), narrow),
            jax.ShapeDtypeStruct((parts, left, width, rows), narrow),
            jax.ShapeDtypeStruct((experts, d_model), narrow),
            jax.ShapeDtypeStruct((3, experts, 1, inner), jnp.float32),
        ),
        in_specs=[any_space] * 5,
        out_specs=(any_space,) * 5 + (pl.BlockSpec(memory_space=pltpu.VMEM),),
        scratch_shapes=[
            pltpu.VMEM((2, rows, inner), jnp.float32),
            pltpu.VMEM((2, rows, inner), jnp.float32),
            pltpu.VMEM((2, inner, rows), jnp.float32),
            pltpu.VMEM((3, 2, inner, rows), narrow),
            pltpu.VMEM((inner, LANES), jnp.float32),
            pltpu.VMEM((3, experts, parts, 1, inner), jnp.float32),
            pltpu.VMEM((experts, rows), jnp.float32),
            pltpu.VMEM((1, rows), jnp.float32),
            pltpu.VMEM((experts, d_model), narrow),
            dma((3, 2)),
            dma((3, parts - 1)),
            dma((3, experts, parts)),
            dma((3, 2, parts - 1)),
            dma((3, experts, parts)),
            dma((3, 2)),
            dma((2, parts)),
            dma((2,)),
            dma((parts - 1,)),
            dma((parts,)),
            dma,
        ],
        compiler_params=pltpu.CompilerParams(collective_id=0, has_side_effects=True),
        name="exchange",
    )(gate, up, down, weight, gain)


def spread_kernel(strip, out, send_sem, recv_sem, own_sem):
    banks = out.shape[0]
    me = lax.axis_index("bank")
    peers = [lax.rem(me + k, banks) for k in range(1, banks)]

    def copy(k, sender):
        return pltpu.make_async_remote_copy(
            src_ref=strip,
            dst_ref=out.at[sender],
            send_sem=send_sem.at[k],
            recv_sem=recv_sem.at[sender],
            device_id={"bank": peers[k]},
            device_id_type=MESH,
        )

    own = pltpu.make_async_copy(strip, out.at[me], own_sem)
    own.start()
    barrier = pltpu.get_barrier_semaphore()
    for peer in peers:
        pl.semaphore_signal(barrier, inc=1, device_id={"bank": peer}, device_id_type=MESH)
    pl.semaphore_wait(barrier, banks - 1)
    for k in range(banks - 1):
        copy(k, me).start()
    for k in range(banks - 1):
        copy(k, me).wait_send()
        copy(k, peers[k]).wait_recv()
    own.wait()


def spread(banks, strip):
    dma = pltpu.SemaphoreType.DMA
    return pl.pallas_call(
        spread_kernel,
        out_shape=jax.ShapeDtypeStruct((banks, *strip.shape), strip.dtype),
        in_specs=[pl.BlockSpec(memory_space=pl.ANY)],
        out_specs=pl.BlockSpec(memory_space=pl.ANY),
        scratch_shapes=[dma((banks - 1,)), dma((banks,)), dma],
        compiler_params=pltpu.CompilerParams(collective_id=1, has_side_effects=True),
        cost_estimate=pl.CostEstimate(
            flops=strip.size, bytes_accessed=4 * banks * strip.size, transcendentals=0
        ),
        name="spread",
    )(strip)


def place_kernel(gate, up, down, router, *refs):
    arrays, stages, (into, out_of) = (gate, up, down, router), refs[4:8], refs[8:]
    pieces = [
        (source.at[e], stage.at[e], result.at[e])
        for source, result, stage in zip(arrays, refs[:4], stages)
        for e in range(source.shape[0])
    ]
    loads = [
        pltpu.make_async_copy(source, stage, into.at[i])
        for i, (source, stage, _) in enumerate(pieces)
    ]
    stores = [
        pltpu.make_async_copy(stage, result, out_of.at[i])
        for i, (_, stage, result) in enumerate(pieces)
    ]
    for copy in loads:
        copy.start()
    for load, store in zip(loads, stores):
        load.wait()
        store.start()
    for copy in stores:
        copy.wait()


def place(*arrays):
    gate, up, down, router = arrays
    results = (gate, up, gate, router)
    pieces = sum(array.shape[0] for array in arrays)
    any_space = pl.BlockSpec(memory_space=pl.ANY)
    moved = sum(array.size for array in arrays)
    return pl.pallas_call(
        place_kernel,
        out_shape=tuple(jax.ShapeDtypeStruct(r.shape, r.dtype) for r in results),
        in_specs=[any_space] * 4,
        out_specs=(any_space,) * 4,
        scratch_shapes=[pltpu.VMEM(array.shape, array.dtype) for array in arrays]
        + [pltpu.SemaphoreType.DMA((pieces,))] * 2,
        cost_estimate=pl.CostEstimate(flops=moved, bytes_accessed=4 * moved, transcendentals=0),
        name="place",
    )(*arrays)


def fill_kernel(blocks, _, out, sem):
    parts, left, _, rows = blocks.shape
    kept = out.shape[0] - left
    copies = [
        pltpu.make_async_copy(
            blocks.at[p, e], out.at[kept + e, :, pl.ds(p * rows, rows)], sem.at[p, e]
        )
        for p in range(parts)
        for e in range(left)
    ]
    for copy in copies:
        copy.start()
    for copy in copies:
        copy.wait()


def fill(blocks, partial):
    parts, left = blocks.shape[:2]
    any_space = pl.BlockSpec(memory_space=pl.ANY)
    return pl.pallas_call(
        fill_kernel,
        out_shape=jax.ShapeDtypeStruct(partial.shape, partial.dtype),
        in_specs=[pl.BlockSpec(memory_space=pltpu.VMEM), any_space],
        out_specs=any_space,
        scratch_shapes=[pltpu.SemaphoreType.DMA((parts, left))],
        input_output_aliases={1: 0},
        compiler_params=pltpu.CompilerParams(vmem_limit_bytes=1 << 20),
        name="fill",
    )(blocks, partial)


def local(parts, banks, master_gate, master_up, master_down, router_weight, router_gain):
    experts, rows, inner = master_gate.shape
    d_model, width = rows * parts, inner // parts
    kept = experts - max(experts // 4, 1)
    *got, cut, strip, scales = exchange(
        parts, kept, master_gate, master_up, master_down,
        router_weight.T, router_gain.reshape(1, rows),
    )
    late = lax.all_to_all(cut, "zero", split_axis=0, concat_axis=0, tiled=True)
    final_gate, final_up, final_down, router = place(*got, spread(banks, strip))
    final_down = fill(late, final_down)
    own = lax.dynamic_slice_in_dim(scales[:, :, 0], lax.axis_index("zero") * width, width, axis=2)
    return (
        final_gate.transpose(0, 2, 1),
        final_up.transpose(0, 2, 1),
        final_down,
        own[GATE],
        own[UP],
        own[DOWN],
        router.reshape(-1, d_model).T,
    )


def solution(mesh):
    placed = (
        P("bank", "zero", None),
        P("bank", "zero", None),
        P("bank", None, "zero"),
        P("zero", "bank"),
        P("zero"),
    )
    parts, banks = mesh.shape["zero"], mesh.shape["bank"]
    return jax.shard_map(
        lambda *arrays: local(parts, banks, *arrays),
        mesh=mesh,
        in_specs=placed,
        out_specs=(
            P("bank", None, "zero"),
            P("bank", None, "zero"),
            P("bank", "zero", None),
            P("bank", "zero"),
            P("bank", "zero"),
            P("bank", "zero"),
            P(),
        ),
        check_vma=False,
    )
```

time: 524 us -> 399 us (0.76)
  Pallas kernels: 0 us -> 391 us
  waiting for transfers between devices: 276 us -> 0.36 us
  blocking collectives: 79.7 us -> 0 us
  local copies, waits for them, and re-layouts: 77.9 us -> 2.11 us
  other arithmetic: 69.2 us -> 0 us
  starting transfers between devices: 18.6 us -> 4.16 us
    pallas_call x0 -> x4, Pallas kernels: none -> 391 us  [the longest x1 359 us: exchange(): pl.pallas_call(functools.partial(exchange_kernel, parts, kept), out_shape...]
    all_to_all x3 -> x1, waiting for transfers between devices: 276 us -> 0.36 us  [local(): late = lax.all_to_all(cut, 'zero', split_axis=0, concat_axis=0, tiled=True)]
    all_gather x2 -> x0, blocking collectives: 79.7 us -> none  [the longest x1 71.1 us: local(): router = lax.all_gather(part_router, ('bank', 'zero'), axis=0, tiled=False)]
    optimization_barrier x2 -> x0, local copies, waits for them, and re-layouts: 46.8 us -> none  [the longest x1 23.4 us: local(): master_gate, cut = lax.optimization_barrier((master_gate, cut))]
    convert_element_type x3 -> x0, other arithmetic: 28.3 us -> none  [exchange(): narrow = (wide / scale[:, :, None]).astype(jnp.bfloat16)]
    reduce_sum x4 -> x0, other arithmetic: 25.3 us -> none  [the longest x1 11 us: local(): jnp.sum(jnp.abs(master_up), axis=1)]
    squeeze x4 -> x0, local copies, waits for them, and re-layouts: 15.3 us -> none  [the longest x3 14.6 us: merged(): return jnp.concatenate([blocks[p] for p in range(blocks.shape[0])], axis=2)]
    transpose x3 -> x0, local copies, waits for them, and re-layouts: 15.1 us -> none  [exchange(): narrow.reshape(experts, parts, rows // parts, width).transpose(1, 0, 2, 3)]
  transfers between devices with their start and end apart: 3 -> 1, of which waited for: 3 -> 1; matrix products, arithmetic and copies ran while one was open for 18% -> 1% of each run, Pallas kernels for 0% -> 8%
where the time goes in v1:
time: 399 us; the launch traced here: 398 us
  Pallas kernels  391 us (98%)
  starting transfers between devices  4.16 us (1%)
    pallas_call x1, Pallas kernels, exchange(): pl.pallas_call(functools.partial(exchange_kernel, parts, kept), out_shape...  359 us
    pallas_call x1, Pallas kernels, place(): pl.pallas_call(place_kernel, out_shape=tuple((jax.ShapeDtypeStruct(r.shap...  21.7 us
    pallas_call x1, Pallas kernels, spread(): pl.pallas_call(spread_kernel, out_shape=jax.ShapeDtypeStruct((banks, *str...  9.04 us
  transfers between devices with their start and end apart: 1, of which 1 were waited for; matrix products, arithmetic and copies ran while one was open for 1% of the time, Pallas kernels for 8%

profile of v1, /device:TPU:0, one launch (start us, length us, event | category | flops | bytes accessed | tf_op | source)
XLA Modules:
  0.0 398.2 jit_solution(17712060942125331641)
XLA Ops:
  0.6 358.6 %exchange.1 = (bf16[8,352,2048]{2,1,0:T(8,128)(2,1)}, bf16[8,352,2048]{2,1,0:T(8,128)(2,1)}, bf16[6,352,2048]{2,1,0:T(8,128)(2,1)}, bf16[4,2,352,512]{3,2,1,0:T(...) custom-call(f32[8,512,1408]{2,1,0:T(8,128)} %gate.1, f32[8,512,1408]{2,1,0:T(8,128)} %up.1, ...), custom_call_target="tpu_custom_call" | custom-call | tf_op jit(solution)/shard_map/exchange/pallas_call | solution.py:295
  359.2 4.2 %all-to-all-start = ((bf16[4,2,352,512]{3,2,1,0:T(8,128)(2,1)}), bf16[4,2,352,512]{3,2,1,0:T(8,128)(2,1)S(1)}, u32[]{:S(2)}, u32[]{:S(2)}) async-start(bf16[4,2,352,512]{3,2,1,0:T(8,128)(2,1)} %get-tuple-element.23), calls=%async_computation | async-start | bytes 5767168 | tf_op jit(solution)/shard_map/all_to_all | solution.py:460
  363.4 9.0 %spread.1.router = bf16[8,8,2048]{2,1,0:T(8,128)(2,1)} custom-call(bf16[8,2048]{1,0:T(8,128)(2,1)} %get-tuple-element.20.strip), custom_call_target="tpu_custom_call" | custom-call | flops 16384 | bytes 524288 | tf_op jit(solution)/shard_map/spread/pallas_call | solution.py:365
  372.4 0.9 constant_dynamic-slice_fusion.2
  373.3 0.6 copy.19
  373.9 21.7 %place.1 = (bf16[8,352,2048]{2,1,0:T(8,128)(2,1)}, bf16[8,352,2048]{2,1,0:T(8,128)(2,1)}, bf16[8,352,2048]{2,1,0:T(8,128)(2,1)}, bf16[8,8,2048]{2,1,0:T(8,128)(2,1)}) custom-call(bf16[8,352,2048]{2,1,0:T(8,128)(2,1)} %get-tuple-element.17.gate, bf16[8,352,2048]{2,1,0:T(8,128)(2,1)} %get-tuple-element.18.up, bf16[6,352,2048]{2,1,0:T(8,128)(2,1)} %get-tuple-element.19.down, ...), custom_call_target="tpu_custom_call" | custom-call | flops 15990784 | bytes 63963136 | tf_op jit(solution)/shard_map/place/pallas_call | solution.py:409
  395.6 0.6 copy_bitcast_fusion
  396.2 0.4 all-to-all-done.blocks
  396.6 1.6 fill.1
Async XLA Ops:
  359.2 37.4 %all-to-all-start = ((bf16[4,2,352,512]{3,2,1,0:T(8,128)(2,1)}), bf16[4,2,352,512]{3,2,1,0:T(8,128)(2,1)S(1)}, u32[]{:S(2)}, u32[]{:S(2)}) async-start(bf16[4,2,352,512]{3,2,1,0:T(8,128)(2,1)} %get-tuple-element.23), calls=%async_computation | async-start | bytes 5767168 | tf_op jit(solution)/shard_map/all_to_all | solution.py:460

commit v2 on v1

--- a/solution.py
+++ b/solution.py
@@ -34,7 +34,7 @@
         put(j, jnp.sum(total.T, axis=0, keepdims=True))
         return 0
 
-    lax.fori_loop(0, wide.shape[0] // LANES, one, 0)
+    lax.fori_loop(0, wide.shape[0] // LANES, one, 0, unroll=True)
 
 
 def exchange_kernel(
@@ -48,31 +48,34 @@
     out_gate,
     out_up,
     out_down,
-    cut,
-    out_strip,
-    scales,
-    wide_gate,
-    wide_up,
-    wide_down,
-    narrow,
-    columns_of,
-    sums,
-    weight_now,
-    gain_now,
-    strip,
-    load_sem,
-    sum_send,
-    sum_recv,
-    data_send,
-    data_recv,
-    own_sem,
-    cut_sem,
-    router_load,
-    part_send,
-    part_recv,
-    strip_sem,
+    *refs,
 ):
-    me = lax.axis_index("zero")
+    cut, (out_router, scales, *refs) = refs[:parts], refs[parts:]
+    (
+        wide_gate,
+        wide_up,
+        wide_down,
+        narrow,
+        columns_of,
+        sums,
+        weight_now,
+        gain_now,
+        strip,
+        load_sem,
+        sum_send,
+        sum_recv,
+        data_send,
+        data_recv,
+        own_sem,
+        cut_sem,
+        router_load,
+        part_send,
+        part_recv,
+        strip_send,
+        strip_recv,
+        strip_own,
+    ) = refs
+    me, here = lax.axis_index("zero"), lax.axis_index("bank")
     experts, rows, inner = gate.shape
     width = inner // parts
     chunk = math.gcd(width, 32)
@@ -80,7 +83,9 @@
     source = {DOWN: down, GATE: gate, UP: up}
     wide = {DOWN: wide_down, GATE: wide_gate, UP: wide_up}
     result = {DOWN: out_down, GATE: out_gate, UP: out_up}
+    banks = out_router.shape[0]
     peers = [lax.rem(me + k, parts) for k in range(1, parts)]
+    others = [lax.rem(here + k, banks) for k in range(1, banks)]
 
     def load(m, e):
         slot = lax.rem(e, 2)
@@ -118,8 +123,8 @@
     def cut_copy(e, p):
         slot = lax.rem(e, 2)
         return pltpu.make_async_copy(
-            narrow.at[DOWN, slot, pl.ds(p * width, width), :],
-            cut.at[p, e - kept],
+            narrow.at[DOWN, slot, span(lax.rem(me + p, parts), width), :],
+            cut[p].at[e - kept],
             cut_sem.at[slot, p],
         )
 
@@ -190,7 +195,7 @@
                         narrow_now[at, lanes] = (wide_now[at, lanes] * inverse).astype(jnp.bfloat16)
                     return 0
 
-                lax.fori_loop(0, width // chunk, one, 0)
+                lax.fori_loop(0, width // chunk, one, 0, unroll=True)
 
             for k in range(parts - 1):
                 scaled(peers[k])
@@ -230,6 +235,17 @@
             device_id_type=MESH,
         )
 
+    def strip_copy(k, sender):
+        return pltpu.make_async_remote_copy(
+            src_ref=strip,
+            dst_ref=out_router.at[sender],
+            send_sem=strip_send.at[k],
+            recv_sem=strip_recv.at[sender],
+            device_id={"bank": others[k]},
+            device_id_type=MESH,
+        )
+
+    own_strip = pltpu.make_async_copy(strip, out_router.at[here], strip_own)
     router_loads = [
         pltpu.make_async_copy(weight, weight_now, router_load.at[0]),
         pltpu.make_async_copy(gain, gain_now, router_load.at[1]),
@@ -241,7 +257,9 @@
     barrier = pltpu.get_barrier_semaphore()
     for peer in peers:
         pl.semaphore_signal(barrier, inc=1, device_id={"zero": peer}, device_id_type=MESH)
-    begin(DOWN, 0, lambda: pl.semaphore_wait(barrier, parts - 1))
+    for other in others:
+        pl.semaphore_signal(barrier, inc=1, device_id={"bank": other}, device_id_type=MESH)
+    begin(DOWN, 0, lambda: pl.semaphore_wait(barrier, parts + banks - 2))
     begin(GATE, 0)
     for copy in router_loads:
         copy.wait()
@@ -257,6 +275,15 @@
         finish(GATE, e)
         pl.when(more)(lambda: begin(GATE, e + 1))
         finish(UP, e)
+
+        @pl.when(e == experts // 2)
+        def _():
+            for k in range(parts - 1):
+                part_copy(k, peers[k]).wait_recv()
+            for k in range(banks - 1):
+                strip_copy(k, here).start()
+            own_strip.start()
+
         return 0
 
     lax.fori_loop(0, experts, step, 0)
@@ -279,13 +306,13 @@
     lax.fori_loop(0, experts, arrived, 0)
     for k in range(parts - 1):
         part_copy(k, me).wait_send()
-        part_copy(k, peers[k]).wait_recv()
-    strip_copy = pltpu.make_async_copy(strip, out_strip, strip_sem)
-    strip_copy.start()
-    strip_copy.wait()
-
-
-def exchange(parts, kept, gate, up, down, weight, gain):
+    for k in range(banks - 1):
+        strip_copy(k, here).wait_send()
+        strip_copy(k, others[k]).wait_recv()
+    own_strip.wait()
+
+
+def exchange(parts, banks, kept, gate, up, down, weight, gain):
     experts, rows, inner = gate.shape
     width, d_model = inner // parts, rows * parts
     left = experts - kept
@@ -298,12 +325,12 @@
             jax.ShapeDtypeStruct((experts, width, d_model), narrow),
             jax.ShapeDtypeStruct((experts, width, d_model), narrow),
             jax.ShapeDtypeStruct((kept, width, d_model), narrow),
-            jax.ShapeDtypeStruct((parts, left, width, rows), narrow),
-            jax.ShapeDtypeStruct((experts, d_model), narrow),
+            *[jax.ShapeDtypeStruct((left, width, rows), narrow)] * parts,
+            jax.ShapeDtypeStruct((banks, experts, d_model), narrow),
             jax.ShapeDtypeStruct((3, experts, 1, inner), jnp.float32),
         ),
         in_specs=[any_space] * 5,
-        out_specs=(any_space,) * 5 + (pl.BlockSpec(memory_space=pltpu.VMEM),),
+        out_specs=(any_space,) * (4 + parts) + (pl.BlockSpec(memory_space=pltpu.VMEM),),
         scratch_shapes=[
             pltpu.VMEM((2, rows, inner), jnp.float32),
             pltpu.VMEM((2, rows, inner), jnp.float32),
@@ -324,6 +351,8 @@
             dma((2,)),
             dma((parts - 1,)),
             dma((parts,)),
+            dma((banks - 1,)),
+            dma((banks,)),
             dma,
         ],
         compiler_params=pltpu.CompilerParams(collective_id=0, has_side_effects=True),
@@ -331,58 +360,20 @@
     )(gate, up, down, weight, gain)
 
 
-def spread_kernel(strip, out, send_sem, recv_sem, own_sem):
-    banks = out.shape[0]
-    me = lax.axis_index("bank")
-    peers = [lax.rem(me + k, banks) for k in range(1, banks)]
-
-    def copy(k, sender):
-        return pltpu.make_async_remote_copy(
-            src_ref=strip,
-            dst_ref=out.at[sender],
-            send_sem=send_sem.at[k],
-            recv_sem=recv_sem.at[sender],
-            device_id={"bank": peers[k]},
-            device_id_type=MESH,
-        )
-
-    own = pltpu.make_async_copy(strip, out.at[me], own_sem)
-    own.start()
-    barrier = pltpu.get_barrier_semaphore()
-    for peer in peers:
-        pl.semaphore_signal(barrier, inc=1, device_id={"bank": peer}, device_id_type=MESH)
-    pl.semaphore_wait(barrier, banks - 1)
-    for k in range(banks - 1):
-        copy(k, me).start()
-    for k in range(banks - 1):
-        copy(k, me).wait_send()
-        copy(k, peers[k]).wait_recv()
-    own.wait()
-
-
-def spread(banks, strip):
-    dma = pltpu.SemaphoreType.DMA
-    return pl.pallas_call(
-        spread_kernel,
-        out_shape=jax.ShapeDtypeStruct((banks, *strip.shape), strip.dtype),
-        in_specs=[pl.BlockSpec(memory_space=pl.ANY)],
-        out_specs=pl.BlockSpec(memory_space=pl.ANY),
-        scratch_shapes=[dma((banks - 1,)), dma((banks,)), dma],
-        compiler_params=pltpu.CompilerParams(collective_id=1, has_side_effects=True),
-        cost_estimate=pl.CostEstimate(
-            flops=strip.size, bytes_accessed=4 * banks * strip.size, transcendentals=0
-        ),
-        name="spread",
-    )(strip)
-
-
-def place_kernel(gate, up, down, router, *refs):
-    arrays, stages, (into, out_of) = (gate, up, down, router), refs[4:8], refs[8:]
+def place_kernel(
+    parts, gate, up, down, router, scales,
+    out_gate, out_up, out_down, out_router, own_gate, own_up, own_down,
+    stage_gate, stage_up, stage_down, stage_router, into, out_of,
+):
     pieces = [
         (source.at[e], stage.at[e], result.at[e])
-        for source, result, stage in zip(arrays, refs[:4], stages)
+        for source, stage, result in (
+            (gate, stage_gate, out_gate),
+            (up, stage_up, out_up),
+            (down, stage_down, out_down),
+        )
         for e in range(source.shape[0])
-    ]
+    ] + [(router, stage_router, out_router)]
     loads = [
         pltpu.make_async_copy(source, stage, into.at[i])
         for i, (source, stage, _) in enumerate(pieces)
@@ -396,36 +387,47 @@
     for load, store in zip(loads, stores):
         load.wait()
         store.start()
+    inner, width = scales.shape[3], own_gate.shape[1]
+    shift = lax.rem(inner - lax.axis_index("zero") * width, inner)
+    for m, own in ((GATE, own_gate), (UP, own_up), (DOWN, own_down)):
+        for e in range(own.shape[0]):
+            own[e : e + 1, :] = pltpu.roll(scales[m, e], shift, 1)[:, :width]
     for copy in stores:
         copy.wait()
 
 
-def place(*arrays):
-    gate, up, down, router = arrays
+def place(parts, gate, up, down, router, scales):
+    arrays = (gate, up, down, router)
     results = (gate, up, gate, router)
-    pieces = sum(array.shape[0] for array in arrays)
-    any_space = pl.BlockSpec(memory_space=pl.ANY)
+    experts, inner = scales.shape[1], scales.shape[3]
+    own = jax.ShapeDtypeStruct((experts, inner // parts), scales.dtype)
+    pieces = gate.shape[0] + up.shape[0] + down.shape[0] + 1
+    any_space, vmem = pl.BlockSpec(memory_space=pl.ANY), pl.BlockSpec(memory_space=pltpu.VMEM)
     moved = sum(array.size for array in arrays)
     return pl.pallas_call(
-        place_kernel,
-        out_shape=tuple(jax.ShapeDtypeStruct(r.shape, r.dtype) for r in results),
-        in_specs=[any_space] * 4,
-        out_specs=(any_space,) * 4,
+        functools.partial(place_kernel, parts),
+        out_shape=tuple(jax.ShapeDtypeStruct(r.shape, r.dtype) for r in results) + (own,) * 3,
+        in_specs=[any_space] * 4 + [vmem],
+        out_specs=(any_space,) * 4 + (vmem,) * 3,
         scratch_shapes=[pltpu.VMEM(array.shape, array.dtype) for array in arrays]
         + [pltpu.SemaphoreType.DMA((pieces,))] * 2,
         cost_estimate=pl.CostEstimate(flops=moved, bytes_accessed=4 * moved, transcendentals=0),
         name="place",
-    )(*arrays)
-
-
-def fill_kernel(blocks, _, out, sem):
-    parts, left, _, rows = blocks.shape
+    )(gate, up, down, router, scales)
+
+
+def fill_kernel(parts, *refs):
+    blocks, out, sem = refs[:parts], refs[parts + 1], refs[parts + 2]
+    me = lax.axis_index("zero")
+    left, _, rows = blocks[0].shape
     kept = out.shape[0] - left
     copies = [
         pltpu.make_async_copy(
-            blocks.at[p, e], out.at[kept + e, :, pl.ds(p * rows, rows)], sem.at[p, e]
-        )
-        for p in range(parts)
+            blocks[k].at[e],
+            out.at[kept + e, :, span(lax.rem(me + parts - k, parts), rows)],
+            sem.at[k, e],
+        )
+        for k in range(parts)
         for e in range(left)
     ]
     for copy in copies:
@@ -435,39 +437,41 @@
 
 
 def fill(blocks, partial):
-    parts, left = blocks.shape[:2]
+    parts, left = len(blocks), blocks[0].shape[0]
     any_space = pl.BlockSpec(memory_space=pl.ANY)
     return pl.pallas_call(
-        fill_kernel,
+        functools.partial(fill_kernel, parts),
         out_shape=jax.ShapeDtypeStruct(partial.shape, partial.dtype),
-        in_specs=[pl.BlockSpec(memory_space=pltpu.VMEM), any_space],
+        in_specs=[pl.BlockSpec(memory_space=pltpu.VMEM)] * parts + [any_space],
         out_specs=any_space,
         scratch_shapes=[pltpu.SemaphoreType.DMA((parts, left))],
-        input_output_aliases={1: 0},
+        input_output_aliases={parts: 0},
         compiler_params=pltpu.CompilerParams(vmem_limit_bytes=1 << 20),
         name="fill",
-    )(blocks, partial)
+    )(*blocks, partial)
 
 
 def local(parts, banks, master_gate, master_up, master_down, router_weight, router_gain):
     experts, rows, inner = master_gate.shape
-    d_model, width = rows * parts, inner // parts
+    d_model = rows * parts
     kept = experts - max(experts // 4, 1)
-    *got, cut, strip, scales = exchange(
-        parts, kept, master_gate, master_up, master_down,
+    got_gate, got_up, got_down, own_cut, *cuts, router, scales = exchange(
+        parts, banks, kept, master_gate, master_up, master_down,
         router_weight.T, router_gain.reshape(1, rows),
     )
-    late = lax.all_to_all(cut, "zero", split_axis=0, concat_axis=0, tiled=True)
-    final_gate, final_up, final_down, router = place(*got, spread(banks, strip))
-    final_down = fill(late, final_down)
-    own = lax.dynamic_slice_in_dim(scales[:, :, 0], lax.axis_index("zero") * width, width, axis=2)
+    late = [
+        lax.ppermute(cut, "zero", [(p, (p + k) % parts) for p in range(parts)])
+        for k, cut in enumerate(cuts, 1)
+    ]
+    final_gate, final_up, final_down, router, *own = place(
+        parts, got_gate, got_up, got_down, router, scales
+    )
+    final_down = fill([own_cut, *late], final_down)
     return (
         final_gate.transpose(0, 2, 1),
         final_up.transpose(0, 2, 1),
         final_down,
-        own[GATE],
-        own[UP],
-        own[DOWN],
+        *own,
         router.reshape(-1, d_model).T,
     )
 

time: 399 us -> 396 us (level)
  Pallas kernels: 391 us -> 384 us
  waiting for transfers between devices: 0.36 us -> 7.11 us
    pallas_call x3 -> x2, Pallas kernels: 32.3 us -> 24.8 us  [the longest x1 23.1 us: place(): pl.pallas_call(functools.partial(place_kernel, parts), out_shape=tuple((j...]
    ppermute x0 -> x3, waiting for transfers between devices: none -> 7.11 us  [local(): lax.ppermute(cut, 'zero', [(p, (p + k) % parts) for p in range(parts)])]
    all_to_all x1 -> x0, starting transfers between devices: 4.16 us -> none  [local(): late = lax.all_to_all(cut, 'zero', split_axis=0, concat_axis=0, tiled=True)]
    ppermute x0 -> x3, starting transfers between devices: none -> 4.13 us  [local(): lax.ppermute(cut, 'zero', [(p, (p + k) % parts) for p in range(parts)])]
  transfers between devices with their start and end apart: 1 -> 3, of which waited for: 1 -> 2; matrix products, arithmetic and copies ran while one was open for 1% -> 0% of each run, Pallas kernels for 8% -> 6%
where the time goes in v2:
time: 396 us
  Pallas kernels  384 us (97%)
  waiting for transfers between devices  7.11 us (2%)
  starting transfers between devices  4.13 us (1%)
    pallas_call x1, Pallas kernels, exchange(): pl.pallas_call(functools.partial(exchange_kernel, parts, kept), out_shape...  359 us
    pallas_call x1, Pallas kernels, place(): pl.pallas_call(functools.partial(place_kernel, parts), out_shape=tuple((j...  23.1 us
  transfers between devices with their start and end apart: 3, of which 2 were waited for; matrix products, arithmetic and copies ran while one was open for 0% of the time, Pallas kernels for 6%

profile of v2, /device:TPU:0, one launch (start us, length us, event | category | flops | bytes accessed | tf_op | source)
XLA Modules:
  0.0 395.6 jit_solution(10545555247122478077)
XLA Ops:
  0.6 359.0 %exchange.1 = (bf16[8,352,2048]{2,1,0:T(8,128)(2,1)}, bf16[8,352,2048]{2,1,0:T(8,128)(2,1)}, bf16[6,352,2048]{2,1,0:T(8,128)(2,1)}, bf16[2,352,512]{2,1,0:T(8,12...) custom-call(f32[8,512,1408]{2,1,0:T(8,128)} %gate.1, ...), custom_call_target="tpu_custom_call" | custom-call | tf_op jit(solution)/shard_map/exchange/pallas_call | solution.py:322
  359.6 2.1 collective-permute-start
  361.7 1.4 collective-permute-start.1
  363.2 0.6 collective-permute-start.2
  363.7 0.0 copy-start
  363.7 23.1 %place.1 = (bf16[8,352,2048]{2,1,0:T(8,128)(2,1)}, bf16[8,352,2048]{2,1,0:T(8,128)(2,1)}, bf16[8,352,2048]{2,1,0:T(8,128)(2,1)}, bf16[8,8,2048]{2,1,0:T(8,128)(2...) custom-call(bf16[8,352,2048]{2,1,0:T(8,128)(2,1)} %get-tuple-element.23.gate, ...), custom_call_target="tpu_custom_call" | custom-call | flops 15990784 | bytes 63963136 | tf_op jit(solution)/shard_map/place/pallas_call | solution.py:407
  386.9 0.0 collective-permute-done.refs_1_
  386.9 6.9 %collective-permute-done.1.refs_2_ = bf16[2,352,512]{2,1,0:T(8,128)(2,1)S(1)} collective-permute-done((bf16[2,352,512]{2,1,0:T(8,128)(2,1)}, bf16[2,352,512]{2,1,0:T(8,128)(2,1)S(1)}, u32[]{:S(2)}, u32[]{:S(2)}) %collective-permute-start.1) | collective-permute-done | bytes 720928 | tf_op jit(solution)/shard_map/ppermute | solution.py:463
  393.8 0.2 collective-permute-done.2.refs_3_
  394.0 0.0 copy-done
  394.0 1.6 fill.1
Async XLA Ops:
  359.6 27.3 %collective-permute-start = (bf16[2,352,512]{2,1,0:T(8,128)(2,1)}, bf16[2,352,512]{2,1,0:T(8,128)(2,1)S(1)}, u32[]{:S(2)}, u32[]{:S(2)}) collective-permute-start(bf16[2,352,512]{2,1,0:T(8,128)(2,1)} %get-tuple-element.31), channel_id=1, source_target_pairs={{0,1},{1,2},{2,3},{3,0},{4,5},{5,6},{6,7},{7,4},{8,9},{9,10},{10,1... | collective-permute-start | bytes 2162696 | tf_op jit(solution)/shard_map/ppermute | solution.py:463
  361.7 32.1 %collective-permute-start.1 = (bf16[2,352,512]{2,1,0:T(8,128)(2,1)}, bf16[2,352,512]{2,1,0:T(8,128)(2,1)S(1)}, u32[]{:S(2)}, u32[]{:S(2)}) collective-permute-start(bf16[2,352,512]{2,1,0:T(8,128)(2,1)} %get-tuple-element.32), channel_id=1, source_target_pairs={{0,2},{1,3},{2,0},{3,1},{4,6},{5,7},{6,4},{7,5},{8,10},{9,11},{10,... | collective-permute-start | bytes 2162696 | tf_op jit(solution)/shard_map/ppermute | solution.py:463
  363.2 30.8 %collective-permute-start.2 = (bf16[2,352,512]{2,1,0:T(8,128)(2,1)}, bf16[2,352,512]{2,1,0:T(8,128)(2,1)S(1)}, u32[]{:S(2)}, u32[]{:S(2)}) collective-permute-start(bf16[2,352,512]{2,1,0:T(8,128)(2,1)} %get-tuple-element.33), channel_id=1, source_target_pairs={{0,3},{1,0},{2,1},{3,2},{4,7},{5,4},{6,5},{7,6},{8,11},{9,8},{10,9... | collective-permute-start | bytes 2162696 | tf_op jit(solution)/shard_map/ppermute | solution.py:463
  363.7 30.3 %copy-start = (bf16[2,352,512]{2,1,0:T(8,128)(2,1)S(1)}, bf16[2,352,512]{2,1,0:T(8,128)(2,1)}, u32[]{:S(2)}) copy-start(bf16[2,352,512]{2,1,0:T(8,128)(2,1)} %get-tuple-element.30.refs_0_) | copy-start | bytes 2162692
